TPU v7x, 32 devices: a whole 2x2x4 slice. The times are simulated.
32 devices in a mesh: gx: 4 (over y, x), gz: 8 (over z, core).
Axes of the slice: x: 2, y: 2, z: 4, core: 2. Of those that a mesh axis runs over, the one named last changes fastest.
Arguments:
- divergence: float32 [256, 128, 512], P('gx', 'gz'), may hold values from -18 to 18
- level_set: float32 [256, 128, 512], P('gx', 'gz'), may hold values from -2 to 2, as said below
- tile_ids: int32 [4, 8192], P('gx', 'gz'), may hold values from -1 to 1023, as said below
Outputs:
- pressure: float32 [256, 128, 512], P('gx', 'gz')
- residual: float32 [256, 128, 512], P('gx', 'gz')
Inputs may be any that keep to these rules, and one draw needn't show every extreme that they name: `level_set`: every entry lies at least 0.05 away from zero. `tile_ids`: each device's part lists distinct tile numbers of its own block, below 1024, in increasing order, followed by -1 entries; some device lists all 1024 and some device lists none.
All inputs are finite; a program needn't handle non-finite values.
Results may differ from a plain program's by a relative error of at most 0.0003.
Values sent between devices are 32-bit elements; how exact they have to be, the bound alone decides.
No kernel may reach another device: no remote copies, remote signals or barrier semaphores. Data moves between devices by JAX's collectives and lax.ppermute only.
A program may use at most 128 MiB of HBM per device.

v0:
```python
import jax
import jax.numpy as jnp
from jax import lax
from jax.sharding import PartitionSpec as P

ITERS = 2
TILE = 8


damping = 2.0 / 3.0
ratio_cap = 20.0


def with_halo(block, sides, width):
    for axis, dim in sides:
        count = lax.axis_size(axis)
        forward = [(i, i + 1) for i in range(count - 1)]
        backward = [(target, source) for source, target in forward]
        low = lax.ppermute(
            lax.slice_in_dim(block, block.shape[dim] - width, None, axis=dim), axis, forward
        )
        high = lax.ppermute(lax.slice_in_dim(block, 0, width, axis=dim), axis, backward)
        block = jnp.concatenate([low, block, high], axis=dim)
    return block


def beside(values):
    center = values[1:-1, 1:-1]
    upward = jnp.concatenate([center[:, :, 1:], jnp.zeros_like(center[:, :, :1])], 2)
    downward = jnp.concatenate([jnp.zeros_like(center[:, :, :1]), center[:, :, :-1]], 2)
    return [
        values[2:, 1:-1],
        values[:-2, 1:-1],
        values[1:-1, 2:],
        values[1:-1, :-2],
        upward,
        downward,
    ]


def beside_all(values):
    pieces = beside(values)
    result = pieces[0] + pieces[1]
    for addend in pieces[2:]:
        result = result + addend
    return result


def coefficients(dist_ext, fluid_ext):
    dist_mid = dist_ext[1:-1, 1:-1]
    fluid_mid = fluid_ext[1:-1, 1:-1]
    safe_dist = jnp.where(dist_mid > 0, dist_mid, 1.0)
    term_list = [
        jnp.where(fluid_side > 0, 1.0, jnp.minimum((dist_mid + dist_side) / safe_dist, ratio_cap))
        for dist_side, fluid_side in zip(beside(dist_ext), beside(fluid_ext))
    ]
    result = term_list[0] + term_list[1]
    for addend in term_list[2:]:
        result = result + addend
    return (jnp.where(fluid_mid > 0, result, 1.0), fluid_mid)


def on_device(divergence, level_set, tile_ids):
    size_x, size_z, size_y = divergence.shape
    tiles_x, tiles_z, tiles_y = (size_x // TILE, size_z // TILE, size_y // TILE)
    listed = tile_ids.reshape(-1)
    numbers = lax.broadcasted_iota(jnp.int32, (1, tiles_x * tiles_z * tiles_y), 1)
    listed_hit = (
        jnp.any(listed[:, None] == numbers, axis=0)
        .astype(jnp.float32)
        .reshape(tiles_x, tiles_z, tiles_y)
    )
    active = jnp.broadcast_to(
        listed_hit[:, None, :, None, :, None], (tiles_x, TILE, tiles_z, TILE, tiles_y, TILE)
    ).reshape(size_x, size_z, size_y)
    fluid_cells = jnp.where(level_set < 0, active, 0.0)
    distance = jnp.abs(level_set)
    stacked = jnp.stack((distance, fluid_cells))
    near_cells = with_halo(stacked, (("gx", 1), ("gz", 2)), 1)
    diag_mid, fluid_mid = coefficients(near_cells[0], near_cells[1])
    scale_mid = damping / diag_mid

    def operate(values):
        padded = with_halo(values, (("gx", 0), ("gz", 1)), 1)
        return fluid_mid * (diag_mid * values - beside_all(padded))

    def precondition(residual):
        first_pass = scale_mid * residual
        second_pass = first_pass + scale_mid * (residual - operate(first_pass))
        return (second_pass, operate(second_pass))

    pressure = jnp.zeros_like(divergence)
    residual = fluid_mid * divergence
    smoothed, precond_image = precondition(residual)
    direction = smoothed
    operated = precond_image

    def both_sums(current, preconditioned, image_of):
        return lax.psum(
            (jnp.sum(current * preconditioned), jnp.sum(image_of * preconditioned)), ("gx", "gz")
        )

    gamma_now, delta_now = both_sums(residual, smoothed, precond_image)
    alpha_now = gamma_now / delta_now
    for iteration in range(ITERS):
        pressure = pressure + alpha_now * direction
        residual = residual - alpha_now * operated
        if iteration + 1 < ITERS:
            smoothed, precond_image = precondition(residual)
            gamma_next, delta_now = both_sums(residual, smoothed, precond_image)
            beta_now = gamma_next / gamma_now
            alpha_now = gamma_next / (delta_now - beta_now * gamma_next / alpha_now)
            direction = smoothed + beta_now * direction
            operated = precond_image + beta_now * operated
            gamma_now = gamma_next
    return (pressure, residual)


def solution(mesh):
    placed = (P("gx", "gz", None), P("gx", "gz", None), P("gx", "gz"))
    return jax.shard_map(
        on_device,
        mesh=mesh,
        in_specs=placed,
        out_specs=(P("gx", "gz", None), P("gx", "gz", None)),
        check_vma=False,
    )
```

profile of v0, /device:TPU:0, one launch (start us, length us, event | category | flops | bytes accessed | tf_op | source)
XLA Modules:
  0.0 272.1 jit_solution(12472779404348531436)
XLA Ops:
  0.6 1.3 fusion
  2.0 11.3 %broadcast_in_dim.18 = f32[8,8,2,8,64,8]{5,4,3,2,1,0:T(8,128)} broadcast(f32[8,2,64]{2,1,0:T(2,128)S(1)} %reshape.16), dimensions={0,2,4} | broadcast | bytes 2101248 | tf_op jit(solution)/shard_map/broadcast_in_dim | solution.py:73
  13.4 25.1 %reshape.15 = f32[64,16,512]{2,1,0:T(8,128)} reshape(f32[8,8,2,8,64,8]{5,4,3,2,1,0:T(8,128)} %broadcast_in_dim.18) | data formatting | bytes 4194304 | tf_op jit(solution)/shard_map/reshape | solution.py:75
  38.4 3.0 %abs_bitcast_fusion = (f32[1,64,16,512]{3,2,1,0:T(8,128)S(1)}, f32[1,64,16,512]{3,2,1,0:T(8,128)S(1)}) fusion(f32[64,16,512]{2,1,0:T(8,128)} %param.4, f32[64,16,512]{2,1,0:T(8,128)} %reshape.15), kind=kLoop, calls=%fused_computation.114 | loop fusion | flops 1572864 | bytes 8388608 | tf_op jit(solution)/shard_map/stack | solution.py:78
  41.4 4.9 %collective-permute-start = (f32[2,1,16,512]{3,2,1,0:T(8,128)S(1)}, f32[2,1,16,512]{3,2,1,0:T(8,128)S(1)}, u32[]{:S(2)}, u32[]{:S(2)}) collective-permute-start(f32[2,1,16,512]{3,2,1,0:T(8,128)S(1)} %get-tuple-element.21), channel_id=1, source_target_pairs={{0,8},{8,16},{16,24},{1,9},{9,17},{17,25},{2,10},{10,18},{18,26},{... | collective-permute-start | bytes 196616 | tf_op jit(solution)/shard_map/ppermute | solution.py:19
  46.3 1.3 collective-permute-start.1
  48.2 4.3 %collective-permute-done.1 = f32[2,1,16,512]{3,2,1,0:T(8,128)S(1)} collective-permute-done((f32[2,1,16,512]{3,2,1,0:T(8,128)S(1)}, f32[2,1,16,512]{3,2,1,0:T(8,128)S(1)}, u32[]{:S(2)}, u32[]{:S(2)}) %collective-permute-start.1) | collective-permute-done | bytes 65568 | tf_op jit(solution)/shard_map/ppermute | solution.py:22
  53.0 1.3 collective-permute-start.2
  54.3 1.3 collective-permute-start.3
  55.6 3.9 %collective-permute-done.3 = f32[2,66,1,512]{3,2,1,0:T(1,128)S(1)} collective-permute-done((f32[2,66,1,512]{3,2,1,0:T(1,128)S(1)}, f32[2,66,1,512]{3,2,1,0:T(1,128)S(1)}, u32[]{:S(2)}, u32[]{:S(2)}) %collective-permute-start.3) | collective-permute-done | bytes 270368 | tf_op jit(solution)/shard_map/ppermute | solution.py:22
  59.6 2.5 pad_maximum_fusion
  62.8 5.4 %fusion.64 = (f32[64,16,511]{2,1,0:T(8,128)}, f32[64,16,511]{2,1,0:T(8,128)}, f32[64,16,511]{2,1,0:T(8,128)}, f32[64,16,511]{2,1,0:T(8,128)}) fusion(f32[66,18,512]{2,1,0:T(8,128)S(1)} %get-tuple-element.17, f32[66,18,512]{2,1,0:T(8,128)S(1)} %get-tuple-element.18), kind=kLoop, calls=%fused_computation.137 | loop fusion | bytes 16744448 | tf_op jit(solution)/shard_map/slice | solution.py:29
  68.2 8.7 %fusion.60 = (f32[64,16,512]{2,1,0:T(8,128)}, f32[64,16,512]{2,1,0:T(8,128)S(1)}, f32[64,16,512]{2,1,0:T(8,128)}) fusion(f32[64,16,511]{2,1,0:T(8,128)} %get-tuple-element.53, f32[64,16,511]{2,1,0:T(8,128)} %get-tuple-element.24, f32[64,16,511]{2,1,0:T(8,128)} %get-tuple-element.54, f32[64,16,511]{2,1,0:T(8,128)} %get-tuple-element.23, ...), kind=kLoop, calls=%fused_computation.118 | loop fusion | flops 22020096 | bytes 37732352 | tf_op jit(solution)/shard_map/mul | solution.py:88
  76.9 1.0 fusion.73
  77.9 4.4 %collective-permute-start.5 = (f32[1,16,512]{2,1,0:T(8,128)S(1)}, f32[1,16,512]{2,1,0:T(8,128)S(1)}, u32[]{:S(2)}, u32[]{:S(2)}) collective-permute-start(f32[1,16,512]{2,1,0:T(8,128)S(1)} %get-tuple-element.49), channel_id=1, source_target_pairs={{0,8},{8,16},{16,24},{1,9},{9,17},{17,25},{2,10},{10,18},{18,26},{... | collective-permute-start | bytes 98312 | tf_op jit(solution)/shard_map/ppermute | solution.py:19
  82.4 1.3 collective-permute-start.4
  83.9 4.2 %collective-permute-done.4 = f32[1,16,512]{2,1,0:T(8,128)S(1)} collective-permute-done((f32[1,16,512]{2,1,0:T(8,128)S(1)}, f32[1,16,512]{2,1,0:T(8,128)S(1)}, u32[]{:S(2)}, u32[]{:S(2)}) %collective-permute-start.4) | collective-permute-done | bytes 32800 | tf_op jit(solution)/shard_map/ppermute | solution.py:22
  88.2 1.8 pad_maximum_fusion.48
  90.0 1.3 collective-permute-start.6
  91.3 6.3 %collective-permute-start.7 = (f32[66,1,512]{2,1,0:T(1,128)S(1)}, f32[66,1,512]{2,1,0:T(1,128)S(1)}, u32[]{:S(2)}, u32[]{:S(2)}) collective-permute-start(f32[66,1,512]{2,1,0:T(1,128)S(1)} %get-tuple-element.34), channel_id=1, source_target_pairs={{0,1},{1,2},{2,3},{3,4},{4,5},{5,6},{6,7},{8,9},{9,10},{10,11},{11... | collective-permute-start | bytes 405512 | tf_op jit(solution)/shard_map/ppermute | solution.py:19
  97.6 0.8 fusion.72
  98.4 4.2 %fusion.32 = f32[64,16,512]{2,1,0:T(8,128)S(1)} fusion(f32[64,16,512]{2,1,0:T(8,128)S(1)} %copy-done.4, f32[64,16,512]{2,1,0:T(8,128)S(1)} %copy-done.7, f32[66,1,512]{2,1,0:T(1,128)S(1)} %collective-permute-done.7, f32[1,16,512]{2,1,0:T(8,128)S(1)} %collective-permute-done.4, f32[1,16,512]{2,1,0:T(8,128)S(1)} %collective-permute-done.5, ...), kind=kLoop, calls=%fused_computation.62 | loop fusion | flops 10485760 | bytes 15007744 | tf_op jit(solution)/shard_map/add | solution.py:89
  102.7 3.4 %collective-permute-start.9 = (f32[1,16,512]{2,1,0:T(8,128)S(1)}, f32[1,16,512]{2,1,0:T(8,128)S(1)}, u32[]{:S(2)}, u32[]{:S(2)}) collective-permute-start(f32[1,16,512]{2,1,0:T(8,128)S(1)} %get-tuple-element.43), channel_id=1, source_target_pairs={{0,8},{8,16},{16,24},{1,9},{9,17},{17,25},{2,10},{10,18},{18,26},{... | collective-permute-start | bytes 98312 | tf_op jit(solution)/shard_map/ppermute | solution.py:19
  106.1 1.3 collective-permute-start.8
  107.7 4.2 %collective-permute-done.8 = f32[1,16,512]{2,1,0:T(8,128)S(1)} collective-permute-done((f32[1,16,512]{2,1,0:T(8,128)S(1)}, f32[1,16,512]{2,1,0:T(8,128)S(1)}, u32[]{:S(2)}, u32[]{:S(2)}) %collective-permute-start.8) | collective-permute-done | bytes 32800 | tf_op jit(solution)/shard_map/ppermute | solution.py:22
  112.2 1.3 collective-permute-start.10
  113.5 3.7 %collective-permute-start.11 = (f32[66,1,512]{2,1,0:T(1,128)S(1)}, f32[66,1,512]{2,1,0:T(1,128)S(1)}, u32[]{:S(2)}, u32[]{:S(2)}) collective-permute-start(f32[66,1,512]{2,1,0:T(1,128)S(1)} %get-tuple-element.32), channel_id=1, source_target_pairs={{0,1},{1,2},{2,3},{3,4},{4,5},{5,6},{6,7},{8,9},{9,10},{10,11},{11... | collective-permute-start | bytes 405512 | tf_op jit(solution)/shard_map/ppermute | solution.py:19
  117.2 0.8 fusion.71
  118.2 5.8 %multiply_reduce_fusion.2 = (f32[]{:T(128)}, f32[]{:T(128)}, f32[64,16,512]{2,1,0:T(8,128)}) fusion(f32[64,16,512]{2,1,0:T(8,128)S(1)} %fusion.32, f32[64,16,512]{2,1,0:T(8,128)S(1)} %copy-done.7, f32[64,16,511]{2,1,0:T(8,128)S(1)} %get-tuple-element.46, f32[64,16,511]{2,1,0:T(8,128)S(1)} %get-tuple-element.45, ...), kind=kLoop, calls=%fused_computation.109 | loop fusion | flops 10485758 | bytes 15007752 | tf_op jit(solution)/shard_map/reduce_sum | solution.py:100
  123.9 45.4 %all-reduce.13 = (f32[]{:T(128)}, f32[]{:T(128)}) all-reduce(f32[]{:T(128)} %get-tuple-element.5, f32[]{:T(128)} %get-tuple-element.4), channel_id=1, replica_groups=mesh['gx'=4,'gz'=8] {'gx','gz'}, use_global_device_ids=true, to_apply=%region_2.3 | all-reduce | flops 2 | bytes 16 | tf_op jit(solution)/shard_map/psum | solution.py:99
  170.6 3.6 %fusion.59 = (f32[64,16,512]{2,1,0:T(8,128)S(1)}, f32[64,16,512]{2,1,0:T(8,128)S(1)}) fusion(f32[64,16,512]{2,1,0:T(8,128)} %copy-done.2, f32[64,16,512]{2,1,0:T(8,128)} %get-tuple-element.16, f32[64,16,512]{2,1,0:T(8,128)} %get-tuple-element.13, f32[]{:T(128)S(6)} %div.44), kind=kLoop, calls=%fused_computation.117 | loop fusion | flops 2097152 | bytes 10485764 | tf_op jit(solution)/shard_map/mul | solution.py:88
  174.2 4.2 %collective-permute-start.13 = (f32[1,16,512]{2,1,0:T(8,128)S(1)}, f32[1,16,512]{2,1,0:T(8,128)S(1)}, u32[]{:S(2)}, u32[]{:S(2)}) collective-permute-start(f32[1,16,512]{2,1,0:T(8,128)S(1)} %get-tuple-element.41), channel_id=1, source_target_pairs={{0,8},{8,16},{16,24},{1,9},{9,17},{17,25},{2,10},{10,18},{18,26},{... | collective-permute-start | bytes 98312 | tf_op jit(solution)/shard_map/ppermute | solution.py:19
  178.4 1.3 collective-permute-start.12
  180.0 4.2 %collective-permute-done.12 = f32[1,16,512]{2,1,0:T(8,128)S(1)} collective-permute-done((f32[1,16,512]{2,1,0:T(8,128)S(1)}, f32[1,16,512]{2,1,0:T(8,128)S(1)}, u32[]{:S(2)}, u32[]{:S(2)}) %collective-permute-start.12) | collective-permute-done | bytes 32800 | tf_op jit(solution)/shard_map/ppermute | solution.py:22
  184.5 1.3 collective-permute-start.14
  185.8 3.2 %collective-permute-start.15 = (f32[66,1,512]{2,1,0:T(1,128)S(1)}, f32[66,1,512]{2,1,0:T(1,128)S(1)}, u32[]{:S(2)}, u32[]{:S(2)}) collective-permute-start(f32[66,1,512]{2,1,0:T(1,128)S(1)} %get-tuple-element.30), channel_id=1, source_target_pairs={{0,1},{1,2},{2,3},{3,4},{4,5},{5,6},{6,7},{8,9},{9,10},{10,11},{11... | collective-permute-start | bytes 405512 | tf_op jit(solution)/shard_map/ppermute | solution.py:19
  189.0 0.8 fusion.68
  190.0 4.2 %fusion.15 = f32[64,16,512]{2,1,0:T(8,128)S(1)} fusion(f32[64,16,512]{2,1,0:T(8,128)S(1)} %get-tuple-element.11, f32[64,16,512]{2,1,0:T(8,128)S(1)} %get-tuple-element.12, f32[66,1,512]{2,1,0:T(1,128)S(1)} %collective-permute-done.15, f32[1,16,512]{2,1,0:T(8,128)S(1)} %collective-permute-done.12, f32[1,16,512]{2,1,0:T(8,128)S(1)} %collective-permute-done.13, ...), kind=kLoop, calls=%fused_computation.29 | loop fusion | flops 10485760 | bytes 15007744 | tf_op jit(solution)/shard_map/add | solution.py:89
  194.2 4.5 %collective-permute-start.17 = (f32[1,16,512]{2,1,0:T(8,128)S(1)}, f32[1,16,512]{2,1,0:T(8,128)S(1)}, u32[]{:S(2)}, u32[]{:S(2)}) collective-permute-start(f32[1,16,512]{2,1,0:T(8,128)S(1)} %get-tuple-element.35), channel_id=1, source_target_pairs={{0,8},{8,16},{16,24},{1,9},{9,17},{17,25},{2,10},{10,18},{18,26},{... | collective-permute-start | bytes 98312 | tf_op jit(solution)/shard_map/ppermute | solution.py:19
  198.7 1.3 collective-permute-start.16
  200.3 4.2 %collective-permute-done.16 = f32[1,16,512]{2,1,0:T(8,128)S(1)} collective-permute-done((f32[1,16,512]{2,1,0:T(8,128)S(1)}, f32[1,16,512]{2,1,0:T(8,128)S(1)}, u32[]{:S(2)}, u32[]{:S(2)}) %collective-permute-start.16) | collective-permute-done | bytes 32800 | tf_op jit(solution)/shard_map/ppermute | solution.py:22
  204.8 1.3 collective-permute-start.18
  206.1 3.4 %collective-permute-start.19 = (f32[66,1,512]{2,1,0:T(1,128)S(1)}, f32[66,1,512]{2,1,0:T(1,128)S(1)}, u32[]{:S(2)}, u32[]{:S(2)}) collective-permute-start(f32[66,1,512]{2,1,0:T(1,128)S(1)} %get-tuple-element.28), channel_id=1, source_target_pairs={{0,1},{1,2},{2,3},{3,4},{4,5},{5,6},{6,7},{8,9},{9,10},{10,11},{11... | collective-permute-start | bytes 405512 | tf_op jit(solution)/shard_map/ppermute | solution.py:19
  209.5 0.8 fusion.67
  210.4 5.8 %multiply_reduce_fusion = (f32[]{:T(128)}, f32[]{:T(128)}, f32[64,16,512]{2,1,0:T(8,128)}) fusion(f32[64,16,512]{2,1,0:T(8,128)S(1)} %fusion.15, f32[64,16,512]{2,1,0:T(8,128)S(1)} %get-tuple-element.12, f32[64,16,511]{2,1,0:T(8,128)S(1)} %get-tuple-element.38, f32[64,16,511]{2,1,0:T(8,128)S(1)} %get-tuple-element.37, ...), kind=kLoop, calls=%fused_computation.106 | loop fusion | flops 10485758 | bytes 15007752 | tf_op jit(solution)/shard_map/reduce_sum | solution.py:100
  216.3 45.0 %all-reduce.12 = (f32[]{:T(128)}, f32[]{:T(128)}) all-reduce(f32[]{:T(128)} %get-tuple-element.3, f32[]{:T(128)} %get-tuple-element.2), channel_id=1, replica_groups=mesh['gx'=4,'gz'=8] {'gx','gz'}, use_global_device_ids=true, to_apply=%region_6.7 | all-reduce | flops 2 | bytes 16 | tf_op jit(solution)/shard_map/psum | solution.py:99
  265.5 4.4 %multiply_add_fusion = f32[64,16,512]{2,1,0:T(8,128)} fusion(f32[64,16,512]{2,1,0:T(8,128)} %copy-done.1, f32[64,16,512]{2,1,0:T(8,128)} %copy-done, f32[]{:T(128)S(6)} %div.45, f32[]{:T(128)S(6)} %div.47, f32[]{:T(128)S(6)} %div.44), kind=kLoop, calls=%fused_computation.105 | loop fusion | flops 2621440 | bytes 6291468 | tf_op jit(solution)/shard_map/add | solution.py:106
  270.0 2.1 multiply_subtract_fusion
  (45 shorter events, 4.2 us)
Async XLA Ops:
  41.4 6.8 %collective-permute-start = (f32[2,1,16,512]{3,2,1,0:T(8,128)S(1)}, f32[2,1,16,512]{3,2,1,0:T(8,128)S(1)}, u32[]{:S(2)}, u32[]{:S(2)}) collective-permute-start(f32[2,1,16,512]{3,2,1,0:T(8,128)S(1)} %get-tuple-element.21), channel_id=1, source_target_pairs={{0,8},{8,16},{16,24},{1,9},{9,17},{17,25},{2,10},{10,18},{18,26},{... | collective-permute-start | bytes 196616 | tf_op jit(solution)/shard_map/ppermute | solution.py:19
  46.3 6.2 %collective-permute-start.1 = (f32[2,1,16,512]{3,2,1,0:T(8,128)S(1)}, f32[2,1,16,512]{3,2,1,0:T(8,128)S(1)}, u32[]{:S(2)}, u32[]{:S(2)}) collective-permute-start(f32[2,1,16,512]{3,2,1,0:T(8,128)S(1)} %get-tuple-element.22), channel_id=1, source_target_pairs={{8,0},{16,8},{24,16},{9,1},{17,9},{25,17},{10,2},{18,10},{26,18},{... | collective-permute-start | bytes 196616 | tf_op jit(solution)/shard_map/ppermute | solution.py:22
  53.0 2.6 collective-permute-start.2
  54.3 5.2 %collective-permute-start.3 = (f32[2,66,1,512]{3,2,1,0:T(1,128)S(1)}, f32[2,66,1,512]{3,2,1,0:T(1,128)S(1)}, u32[]{:S(2)}, u32[]{:S(2)}) collective-permute-start(f32[2,66,1,512]{3,2,1,0:T(1,128)S(1)} %get-tuple-element.20), channel_id=1, source_target_pairs={{1,0},{2,1},{3,2},{4,3},{5,4},{6,5},{7,6},{9,8},{10,9},{11,10},{12... | collective-permute-start | bytes 811016 | tf_op jit(solution)/shard_map/ppermute | solution.py:22
  76.9 41.3 %copy-start.2 = (f32[64,16,512]{2,1,0:T(8,128)}, f32[64,16,512]{2,1,0:T(8,128)S(1)}, u32[]{:S(2)}) copy-start(f32[64,16,512]{2,1,0:T(8,128)S(1)} %get-tuple-element.15) | copy-start | bytes 6291460
  76.9 20.6 %copy-start.4 = (f32[64,16,512]{2,1,0:T(8,128)S(1)}, f32[64,16,512]{2,1,0:T(8,128)}, u32[]{:S(2)}) copy-start(f32[64,16,512]{2,1,0:T(8,128)} %get-tuple-element.14) | copy-start | bytes 6291460
  77.9 6.0 %collective-permute-start.5 = (f32[1,16,512]{2,1,0:T(8,128)S(1)}, f32[1,16,512]{2,1,0:T(8,128)S(1)}, u32[]{:S(2)}, u32[]{:S(2)}) collective-permute-start(f32[1,16,512]{2,1,0:T(8,128)S(1)} %get-tuple-element.49), channel_id=1, source_target_pairs={{0,8},{8,16},{16,24},{1,9},{9,17},{17,25},{2,10},{10,18},{18,26},{... | collective-permute-start | bytes 98312 | tf_op jit(solution)/shard_map/ppermute | solution.py:19
  82.4 5.8 %collective-permute-start.4 = (f32[1,16,512]{2,1,0:T(8,128)S(1)}, f32[1,16,512]{2,1,0:T(8,128)S(1)}, u32[]{:S(2)}, u32[]{:S(2)}) collective-permute-start(f32[1,16,512]{2,1,0:T(8,128)S(1)} %get-tuple-element.50), channel_id=1, source_target_pairs={{8,0},{16,8},{24,16},{9,1},{17,9},{25,17},{10,2},{18,10},{26,18},{... | collective-permute-start | bytes 98312 | tf_op jit(solution)/shard_map/ppermute | solution.py:22
  90.0 8.4 %collective-permute-start.6 = (f32[66,1,512]{2,1,0:T(1,128)S(1)}, f32[66,1,512]{2,1,0:T(1,128)S(1)}, u32[]{:S(2)}, u32[]{:S(2)}) collective-permute-start(f32[66,1,512]{2,1,0:T(1,128)S(1)} %get-tuple-element.33), channel_id=1, source_target_pairs={{1,0},{2,1},{3,2},{4,3},{5,4},{6,5},{7,6},{9,8},{10,9},{11,10},{12... | collective-permute-start | bytes 405512 | tf_op jit(solution)/shard_map/ppermute | solution.py:22
  91.3 7.1 %copy-start.7 = (f32[64,16,512]{2,1,0:T(8,128)S(1)}, f32[64,16,512]{2,1,0:T(8,128)}, u32[]{:S(2)}) copy-start(f32[64,16,512]{2,1,0:T(8,128)} %get-tuple-element.16) | copy-start | bytes 6291460
  91.3 7.1 %collective-permute-start.7 = (f32[66,1,512]{2,1,0:T(1,128)S(1)}, f32[66,1,512]{2,1,0:T(1,128)S(1)}, u32[]{:S(2)}, u32[]{:S(2)}) collective-permute-start(f32[66,1,512]{2,1,0:T(1,128)S(1)} %get-tuple-element.34), channel_id=1, source_target_pairs={{0,1},{1,2},{2,3},{3,4},{4,5},{5,6},{6,7},{8,9},{9,10},{10,11},{11... | collective-permute-start | bytes 405512 | tf_op jit(solution)/shard_map/ppermute | solution.py:19
  102.7 15.5 %copy-start = (f32[64,16,512]{2,1,0:T(8,128)}, f32[64,16,512]{2,1,0:T(8,128)S(1)}, u32[]{:S(2)}) copy-start(f32[64,16,512]{2,1,0:T(8,128)S(1)} %fusion.32) | copy-start | bytes 6291460
  102.7 5.0 %collective-permute-start.9 = (f32[1,16,512]{2,1,0:T(8,128)S(1)}, f32[1,16,512]{2,1,0:T(8,128)S(1)}, u32[]{:S(2)}, u32[]{:S(2)}) collective-permute-start(f32[1,16,512]{2,1,0:T(8,128)S(1)} %get-tuple-element.43), channel_id=1, source_target_pairs={{0,8},{8,16},{16,24},{1,9},{9,17},{17,25},{2,10},{10,18},{18,26},{... | collective-permute-start | bytes 98312 | tf_op jit(solution)/shard_map/ppermute | solution.py:19
  106.1 5.8 %collective-permute-start.8 = (f32[1,16,512]{2,1,0:T(8,128)S(1)}, f32[1,16,512]{2,1,0:T(8,128)S(1)}, u32[]{:S(2)}, u32[]{:S(2)}) collective-permute-start(f32[1,16,512]{2,1,0:T(8,128)S(1)} %get-tuple-element.44), channel_id=1, source_target_pairs={{8,0},{16,8},{24,16},{9,1},{17,9},{25,17},{10,2},{18,10},{26,18},{... | collective-permute-start | bytes 98312 | tf_op jit(solution)/shard_map/ppermute | solution.py:22
  112.2 5.9 %collective-permute-start.10 = (f32[66,1,512]{2,1,0:T(1,128)S(1)}, f32[66,1,512]{2,1,0:T(1,128)S(1)}, u32[]{:S(2)}, u32[]{:S(2)}) collective-permute-start(f32[66,1,512]{2,1,0:T(1,128)S(1)} %get-tuple-element.31), channel_id=1, source_target_pairs={{1,0},{2,1},{3,2},{4,3},{5,4},{6,5},{7,6},{9,8},{10,9},{11,10},{12... | collective-permute-start | bytes 405512 | tf_op jit(solution)/shard_map/ppermute | solution.py:22
  113.5 4.7 %collective-permute-start.11 = (f32[66,1,512]{2,1,0:T(1,128)S(1)}, f32[66,1,512]{2,1,0:T(1,128)S(1)}, u32[]{:S(2)}, u32[]{:S(2)}) collective-permute-start(f32[66,1,512]{2,1,0:T(1,128)S(1)} %get-tuple-element.32), channel_id=1, source_target_pairs={{0,1},{1,2},{2,3},{3,4},{4,5},{5,6},{6,7},{8,9},{9,10},{10,11},{11... | collective-permute-start | bytes 405512 | tf_op jit(solution)/shard_map/ppermute | solution.py:19
  174.2 36.2 %copy-start.5 = (f32[64,16,512]{2,1,0:T(8,128)}, f32[64,16,512]{2,1,0:T(8,128)S(1)}, u32[]{:S(2)}) copy-start(f32[64,16,512]{2,1,0:T(8,128)S(1)} %get-tuple-element.12) | copy-start | bytes 6291460
  174.2 5.8 %collective-permute-start.13 = (f32[1,16,512]{2,1,0:T(8,128)S(1)}, f32[1,16,512]{2,1,0:T(8,128)S(1)}, u32[]{:S(2)}, u32[]{:S(2)}) collective-permute-start(f32[1,16,512]{2,1,0:T(8,128)S(1)} %get-tuple-element.41), channel_id=1, source_target_pairs={{0,8},{8,16},{16,24},{1,9},{9,17},{17,25},{2,10},{10,18},{18,26},{... | collective-permute-start | bytes 98312 | tf_op jit(solution)/shard_map/ppermute | solution.py:19
  178.4 5.8 %collective-permute-start.12 = (f32[1,16,512]{2,1,0:T(8,128)S(1)}, f32[1,16,512]{2,1,0:T(8,128)S(1)}, u32[]{:S(2)}, u32[]{:S(2)}) collective-permute-start(f32[1,16,512]{2,1,0:T(8,128)S(1)} %get-tuple-element.42), channel_id=1, source_target_pairs={{8,0},{16,8},{24,16},{9,1},{17,9},{25,17},{10,2},{18,10},{26,18},{... | collective-permute-start | bytes 98312 | tf_op jit(solution)/shard_map/ppermute | solution.py:22
  184.5 5.3 %collective-permute-start.14 = (f32[66,1,512]{2,1,0:T(1,128)S(1)}, f32[66,1,512]{2,1,0:T(1,128)S(1)}, u32[]{:S(2)}, u32[]{:S(2)}) collective-permute-start(f32[66,1,512]{2,1,0:T(1,128)S(1)} %get-tuple-element.29), channel_id=1, source_target_pairs={{1,0},{2,1},{3,2},{4,3},{5,4},{6,5},{7,6},{9,8},{10,9},{11,10},{12... | collective-permute-start | bytes 405512 | tf_op jit(solution)/shard_map/ppermute | solution.py:22
  185.8 4.2 %copy-start.3 = (f32[64,16,512]{2,1,0:T(8,128)S(1)}, f32[64,16,512]{2,1,0:T(8,128)}, u32[]{:S(2)}) copy-start(f32[64,16,512]{2,1,0:T(8,128)} %copy-done.2) | copy-start | bytes 6291460
  185.8 4.1 %collective-permute-start.15 = (f32[66,1,512]{2,1,0:T(1,128)S(1)}, f32[66,1,512]{2,1,0:T(1,128)S(1)}, u32[]{:S(2)}, u32[]{:S(2)}) collective-permute-start(f32[66,1,512]{2,1,0:T(1,128)S(1)} %get-tuple-element.30), channel_id=1, source_target_pairs={{0,1},{1,2},{2,3},{3,4},{4,5},{5,6},{6,7},{8,9},{9,10},{10,11},{11... | collective-permute-start | bytes 405512 | tf_op jit(solution)/shard_map/ppermute | solution.py:19
  194.2 16.2 %copy-start.1 = (f32[64,16,512]{2,1,0:T(8,128)}, f32[64,16,512]{2,1,0:T(8,128)S(1)}, u32[]{:S(2)}) copy-start(f32[64,16,512]{2,1,0:T(8,128)S(1)} %fusion.15) | copy-start | bytes 6291460
  194.2 6.1 %collective-permute-start.17 = (f32[1,16,512]{2,1,0:T(8,128)S(1)}, f32[1,16,512]{2,1,0:T(8,128)S(1)}, u32[]{:S(2)}, u32[]{:S(2)}) collective-permute-start(f32[1,16,512]{2,1,0:T(8,128)S(1)} %get-tuple-element.35), channel_id=1, source_target_pairs={{0,8},{8,16},{16,24},{1,9},{9,17},{17,25},{2,10},{10,18},{18,26},{... | collective-permute-start | bytes 98312 | tf_op jit(solution)/shard_map/ppermute | solution.py:19
  198.7 5.8 %collective-permute-start.16 = (f32[1,16,512]{2,1,0:T(8,128)S(1)}, f32[1,16,512]{2,1,0:T(8,128)S(1)}, u32[]{:S(2)}, u32[]{:S(2)}) collective-permute-start(f32[1,16,512]{2,1,0:T(8,128)S(1)} %get-tuple-element.36), channel_id=1, source_target_pairs={{8,0},{16,8},{24,16},{9,1},{17,9},{25,17},{10,2},{18,10},{26,18},{... | collective-permute-start | bytes 98312 | tf_op jit(solution)/shard_map/ppermute | solution.py:22
  204.8 5.6 %collective-permute-start.18 = (f32[66,1,512]{2,1,0:T(1,128)S(1)}, f32[66,1,512]{2,1,0:T(1,128)S(1)}, u32[]{:S(2)}, u32[]{:S(2)}) collective-permute-start(f32[66,1,512]{2,1,0:T(1,128)S(1)} %get-tuple-element.27), channel_id=1, source_target_pairs={{1,0},{2,1},{3,2},{4,3},{5,4},{6,5},{7,6},{9,8},{10,9},{11,10},{12... | collective-permute-start | bytes 405512 | tf_op jit(solution)/shard_map/ppermute | solution.py:22
  206.1 4.3 %collective-permute-start.19 = (f32[66,1,512]{2,1,0:T(1,128)S(1)}, f32[66,1,512]{2,1,0:T(1,128)S(1)}, u32[]{:S(2)}, u32[]{:S(2)}) collective-permute-start(f32[66,1,512]{2,1,0:T(1,128)S(1)} %get-tuple-element.28), channel_id=1, source_target_pairs={{0,1},{1,2},{2,3},{3,4},{4,5},{5,6},{6,7},{8,9},{9,10},{10,11},{11... | collective-permute-start | bytes 405512 | tf_op jit(solution)/shard_map/ppermute | solution.py:19
  265.5 4.5 %copy-start.6 = (f32[64,16,512]{2,1,0:T(8,128)S(1)}, f32[64,16,512]{2,1,0:T(8,128)}, u32[]{:S(2)}) copy-start(f32[64,16,512]{2,1,0:T(8,128)} %copy-done.5) | copy-start | bytes 6291460
  265.5 4.4 %copy-start.8 = (f32[64,16,512]{2,1,0:T(8,128)S(1)}, f32[64,16,512]{2,1,0:T(8,128)}, u32[]{:S(2)}) copy-start(f32[64,16,512]{2,1,0:T(8,128)} %get-tuple-element.13) | copy-start | bytes 6291460
  265.5 4.4 %copy-start.9 = (f32[64,16,512]{2,1,0:T(8,128)S(1)}, f32[64,16,512]{2,1,0:T(8,128)}, u32[]{:S(2)}) copy-start(f32[64,16,512]{2,1,0:T(8,128)} %get-tuple-element.10) | copy-start | bytes 6291460
where the time goes:
time: 273 us; the launch traced here: 272 us
  blocking collectives  90.4 us (33%)
  starting transfers between devices  52.2 us (19%)
  other arithmetic  48.8 us (18%)
  local copies, waits for them, and re-layouts  47 us (17%)
  waiting for transfers between devices  27.1 us (10%)
  between operations  6.58 us (2%)
    psum x2, blocking collectives, both_sums(): lax.psum((jnp.sum(current * preconditioned), jnp.sum(image_of * precondit...  90.4 us
    ppermute x10, starting transfers between devices, with_halo(): lax.ppermute(lax.slice_in_dim(block, block.shape[dim] - width, None, axis...  39.3 us
    ppermute x10, waiting for transfers between devices, with_halo(): lax.ppermute(lax.slice_in_dim(block, 0, width, axis=dim), axis, backward)  25.1 us
    reshape x1, local copies, waits for them, and re-layouts, on_device(): active = jnp.broadcast_to(listed_hit[:, None, :, None, :, None], (tiles_x...  25.1 us
    ppermute x10, starting transfers between devices, with_halo(): lax.ppermute(lax.slice_in_dim(block, 0, width, axis=dim), axis, backward)  12.9 us
    mul x2, other arithmetic, precondition(): first_pass = scale_mid * residual  12.3 us
    reduce_sum x2, other arithmetic, both_sums(): jnp.sum(image_of * preconditioned)  11.6 us
    broadcast_in_dim x1, local copies, waits for them, and re-layouts, on_device(): jnp.broadcast_to(listed_hit[:, None, :, None, :, None], (tiles_x, TILE, t...  11.3 us
  transfers between devices with their start and end apart: 20, of which 13 were waited for; matrix products, arithmetic and copies ran while one was open for 1% of the time, Pallas kernels for 0%

commit v1 on v0

v1 whole, which is shorter than its diff:
```python
import functools

import jax
import jax.numpy as jnp
from jax import lax
from jax.experimental import pallas as pl
from jax.experimental.pallas import tpu as pltpu
from jax.sharding import PartitionSpec as P


TILE = 8
LANES = 128
HALO = 4
DEEP = HALO + 1
damping = 2.0 / 3.0
ratio_cap = 20.0
f32 = jnp.float32

VMEM_SPEC = pl.BlockSpec(memory_space=pltpu.VMEM)
HBM_SPEC = pl.BlockSpec(memory_space=pltpu.HBM)


ORIGIN = 12
ROWS = 24
RING = 16


def limit(mib):
    return pltpu.CompilerParams(vmem_limit_bytes=mib << 20)


def array(*shape):
    return jax.ShapeDtypeStruct(shape, f32)


def by_parity(axis, body):
    odd = lax.rem(lax.axis_index(axis), 2)

    @pl.when(odd == 0)
    def _():
        body(0)

    @pl.when(odd == 1)
    def _():
        body(1)


def flags_kernel(dims, ids_ref, act_ref):
    size_x, size_z, size_y = dims
    tiles_x, tiles_z, tiles_y = size_x // TILE, size_z // TILE, size_y // TILE
    ids = ids_ref[...]
    slots = ids.shape[1]
    column = lax.div(lax.broadcasted_iota(jnp.int32, (size_y, slots), 0), TILE)
    along_y = (column == lax.rem(ids, tiles_y)).astype(f32).astype(jnp.bfloat16)
    first = lax.broadcasted_iota(jnp.int32, (tiles_x, slots), 0) * (tiles_z * tiles_y)
    for layer in range(tiles_z):
        low = first + layer * tiles_y
        mine = jnp.logical_and(ids >= low, ids < low + tiles_y).astype(f32).astype(jnp.bfloat16)
        act_ref[layer] = lax.dot_general(
            mine, along_y, (((1,), (1,)), ((), ())), preferred_element_type=f32
        )


def pair(first_rows, low_ls, high_ls, low_div, high_div):
    up = jnp.where(first_rows, pltpu.roll(high_div, HALO, 0), high_ls)
    down = jnp.where(first_rows, low_ls, pltpu.roll(low_div, HALO, 0))
    return up, down


def pack_x_kernel(dims, ids_hbm, ls_hbm, div_hbm, even_ref, odd_ref, act_ref, ids, buf, sems):
    size_x, size_z, _ = dims
    tiles_x, tiles_z = size_x // TILE, size_z // TILE
    ids_copy = pltpu.make_async_copy(ids_hbm, ids, sems.at[4])
    ids_copy.start()
    copies = []
    for source, first, count, place in (
        (ls_hbm, size_x - DEEP, DEEP, 0),
        (div_hbm, size_x - HALO, HALO, DEEP),
        (ls_hbm, 0, DEEP, DEEP + HALO),
        (div_hbm, 0, HALO, 2 * DEEP + HALO),
    ):
        copy = pltpu.make_async_copy(
            source.at[pl.ds(first, count)], buf.at[pl.ds(place, count)], sems.at[len(copies)]
        )
        copy.start()
        copies.append(copy)
    ids_copy.wait()
    flags_kernel(dims, ids, act_ref)
    for copy in copies:
        copy.wait()

    def put(odd):
        for ref, place, tile_x in zip((even_ref, odd_ref), (odd, 1 - odd), (0, 0)):
            tile_x = tiles_x - 1 if place == 0 else 0
            for p in range(DEEP + HALO):
                ref[p * size_z : (p + 1) * size_z] = buf[place * (DEEP + HALO) + p]
            flags = (DEEP + HALO) * size_z
            for layer in range(tiles_z):
                ref[flags + layer : flags + layer + 1] = act_ref[layer, tile_x : tile_x + 1]

    by_parity("gx", put)


def pack_z_kernel(dims, parts, ls_ref, div_ref, act_ref, *refs):
    _, size_z, size_y = dims
    tiles_z = size_z // TILE
    first_rows = lax.broadcasted_iota(jnp.int32, (TILE, size_y), 0) < HALO
    top = slice(size_z - TILE, size_z)

    def put(odd):
        for part, (base, span) in enumerate(parts):
            even_ref, odd_ref = refs[2 * part], refs[2 * part + 1]
            up_z, down_z = (even_ref, odd_ref) if odd == 0 else (odd_ref, even_ref)

            def planes(x0, carry):
                fifth_up, fifth_down = [], []
                for p in range(TILE):
                    x = base + x0 * TILE + p
                    low_ls, high_ls = ls_ref[x, 0:TILE], ls_ref[x, top]
                    up, down = pair(first_rows, low_ls, high_ls, div_ref[x, 0:TILE], div_ref[x, top])
                    row = pl.multiple_of((x - base) * TILE, TILE)
                    up_z[pl.ds(row, TILE)] = up
                    down_z[pl.ds(row, TILE)] = down
                    fifth_up.append(high_ls[TILE - DEEP : TILE - HALO])
                    fifth_down.append(low_ls[HALO:DEEP])
                row = pl.multiple_of((span + x0) * TILE, TILE)
                up_z[pl.ds(row, TILE)] = jnp.concatenate(fifth_up, 0)
                down_z[pl.ds(row, TILE)] = jnp.concatenate(fifth_down, 0)
                return carry

            lax.fori_loop(0, span // TILE, planes, 0)
            flags, tiles = span * (TILE + 1), slice(base // TILE, (base + span) // TILE)
            up_z[flags : flags + span // TILE] = act_ref[tiles_z - 1, tiles]
            down_z[flags : flags + span // TILE] = act_ref[0, tiles]

    by_parity("gz", put)


def pack_corner_kernel(dims, x_even, x_odd, after_ref, even_ref, odd_ref):
    del after_ref
    _, size_z, size_y = dims
    tiles_z = size_z // TILE
    first_rows = lax.broadcasted_iota(jnp.int32, (TILE, size_y), 0) < HALO
    flags = (DEEP + HALO) * size_z

    def put(odd_x):
        low, high = (x_odd, x_even) if odd_x == 0 else (x_even, x_odd)

        def put_z(odd_z):
            up_ref, down_ref = (even_ref, odd_ref) if odd_z == 0 else (odd_ref, even_ref)
            for side, ref in enumerate((low, high)):
                for p in range(HALO):
                    ls_row = (p + 1 - side) * size_z
                    div_row = (DEEP + p) * size_z
                    up, down = pair(
                        first_rows,
                        ref[ls_row : ls_row + TILE],
                        ref[ls_row + size_z - TILE : ls_row + size_z],
                        ref[div_row : div_row + TILE],
                        ref[div_row + size_z - TILE : div_row + size_z],
                    )
                    row = (side * HALO + p) * TILE
                    up_ref[row : row + TILE] = up
                    down_ref[row : row + TILE] = down
                row = 2 * HALO * TILE + side
                up_ref[row : row + 1] = ref[flags + tiles_z - 1 : flags + tiles_z]
                down_ref[row : row + 1] = ref[flags : flags + 1]

        by_parity("gz", put_z)

    by_parity("gx", put)


class Stages:
    def __init__(self, dims, ring, open_ref, dist_ref, src_ref, gain_ref, va_ref, vb_ref, u_ref):
        self.ring = ring
        self.size_x, self.size_z, self.size_y = dims
        self.count = self.size_y // LANES
        self.open, self.dist, self.src, self.gain = open_ref, dist_ref, src_ref, gain_ref
        self.va, self.vb, self.u = va_ref, vb_ref, u_ref
        self.low, self.wide = ORIGIN - HALO, self.size_z + 2 * HALO
        self.tile_rows = lax.broadcasted_iota(jnp.int32, (TILE, self.size_y), 0)

    def at(self, slot):
        return jnp.bitwise_and(slot, self.ring - 1) if self.ring else slot

    def chunk(self, c):
        return slice(c * LANES, (c + 1) * LANES)

    def put(self, slot, row, levels, act):
        slot = self.at(slot)
        fluid = jnp.logical_and(levels < 0, act > 0)
        away = jnp.abs(levels)
        opened = jnp.where(fluid, 0.0, away)
        dist = jnp.where(fluid, away, 0.0)
        for c in range(self.count):
            self.open[slot, c, row : row + TILE] = opened[:, self.chunk(c)]
            self.dist[slot, c, row : row + TILE] = dist[:, self.chunk(c)]

    def put_source(self, slot, row, values):
        slot = self.at(slot)
        for c in range(self.count):
            self.src[slot, c, row : row + values.shape[0]] = values[:, self.chunk(c)]

    def spread(self, row):
        return jnp.broadcast_to(row, (TILE, self.size_y))

    def own_plane(self, slot, x, ls_ref, div_ref, act_ref, zl_ref, zh_ref, base, span):
        size_z = self.size_z
        tile_x = lax.div(x, TILE)
        row = (x - base) * TILE
        row = row if isinstance(x, int) else pl.multiple_of(row, TILE)
        flag, fifth = span * (TILE + 1) + tile_x - base // TILE, span * TILE + x - base
        below, above = zl_ref[pl.ds(row, TILE)], zh_ref[pl.ds(row, TILE)]
        self.put_source(slot, ORIGIN - HALO, below)
        self.put_source(slot, ORIGIN + size_z - HALO, above)
        self.put_source(slot, ORIGIN, div_ref[x])
        below = jnp.where(self.tile_rows == HALO - 1, self.spread(zl_ref[pl.ds(fifth, 1)]), below)
        above = jnp.where(self.tile_rows == HALO, self.spread(zh_ref[pl.ds(fifth, 1)]), above)
        self.put(slot, ORIGIN - TILE, below, self.spread(zl_ref[pl.ds(flag, 1)]))
        self.put(slot, ORIGIN + size_z, above, self.spread(zh_ref[pl.ds(flag, 1)]))
        for j in range(size_z // TILE):
            rows = slice(j * TILE, (j + 1) * TILE)
            self.put(slot, ORIGIN + j * TILE, ls_ref[x, rows], self.spread(act_ref[j, pl.ds(tile_x, 1)]))

    def lateral(self, values):
        lane = lax.broadcasted_iota(jnp.int32, values[0].shape, 1)
        first, last = lane == 0, lane == LANES - 1
        left = [pltpu.roll(v, 1, 1) for v in values]
        right = [pltpu.roll(v, LANES - 1, 1) for v in values]
        lefts = [jnp.where(first, left[c - 1] if c else 0.0, left[c]) for c in range(self.count)]
        rights = [
            jnp.where(last, right[c + 1] if c + 1 < self.count else 0.0, right[c])
            for c in range(self.count)
        ]
        return lefts, rights

    def near(self, ref, slot, low, wide):
        rows = slice(low, low + wide)
        here, before, after = self.at(slot), self.at(slot - 1), self.at(slot + 1)
        lefts, rights = self.lateral([ref[here, c, rows] for c in range(self.count)])
        return [
            (ref[after, c, rows] + ref[before, c, rows])
            + (ref[here, c, low + 1 : low + wide + 1] + ref[here, c, low - 1 : low + wide - 1])
            + (lefts[c] + rights[c])
            for c in range(self.count)
        ]

    def gains(self, slot):
        low, wide, ref = self.low, self.wide, self.open
        rows = slice(low, low + wide)
        before, after, slot = self.at(slot - 1), self.at(slot + 1), self.at(slot)
        lefts, rights = self.lateral([ref[slot, c, rows] for c in range(self.count)])
        for c in range(self.count):
            dist = self.dist[slot, c, rows]
            top = (ratio_cap - 1.0) * dist
            pieces = [
                jnp.minimum(piece, top)
                for piece in (
                    ref[after, c, rows],
                    ref[before, c, rows],
                    ref[slot, c, low + 1 : low + wide + 1],
                    ref[slot, c, low - 1 : low + wide - 1],
                    lefts[c],
                    rights[c],
                )
            ]
            total = (pieces[0] + pieces[1]) + (pieces[2] + pieces[3]) + (pieces[4] + pieces[5])
            whole = jnp.where(dist > 0, 6.0 * dist + total, 1.0)
            gain = damping * dist / whole
            self.gain[slot, c, rows] = gain
            self.va[slot, c, rows] = gain * self.src[slot, c, rows]

    def smooth_first(self, slot):
        rows = slice(self.low, self.low + self.wide)
        around = self.near(self.va, slot, self.low, self.wide)
        slot = self.at(slot)
        for c in range(self.count):
            u = (2.0 * damping) * self.src[slot, c, rows] + around[c]
            self.u[slot, c, rows] = u
            self.vb[slot, c, rows] = self.gain[slot, c, rows] * u

    def image_first(self, slot):
        rows = slice(self.low, self.low + self.wide)
        around = self.near(self.vb, slot, self.low, self.wide)
        slot = self.at(slot)
        for c in range(self.count):
            w = damping * self.u[slot, c, rows] - around[c]
            self.u[slot, c, rows] = w
            self.va[slot, c, rows] = self.gain[slot, c, rows] * w

    def keep_first(self, slot, x, place, div_ref, z_out, r_out, w_out, dots):
        own = slice(ORIGIN, ORIGIN + self.size_z)
        slot = self.at(slot)
        gamma, delta = [], []
        for c in range(self.count):
            ch = self.chunk(c)
            fluid = self.gain[slot, c, own] > 0
            z = self.vb[slot, c, own]
            r = jnp.where(fluid, div_ref[x, :, ch], 0.0)
            w = jnp.where(fluid, self.u[slot, c, own], 0.0)
            z_out[place + (slice(None), ch)] = z
            r_out[place + (slice(None), ch)] = r
            w_out[place + (slice(None), ch)] = w
            gamma.append(r * z)
            delta.append(z * w)
        dots[0] += self.folded(gamma)
        dots[1] += self.folded(delta)

    def smooth_second(self, slot):
        rows = slice(self.low, self.low + self.wide)
        around = self.near(self.va, slot, self.low, self.wide)
        slot = self.at(slot)
        for c in range(self.count):
            u = (2.0 * damping) * self.u[slot, c, rows] + around[c]
            self.u[slot, c, rows] = u
            self.vb[slot, c, rows] = self.gain[slot, c, rows] * u

    def image_second(self, slot, place, w_ref, w_place, q_out, t_out, dots):
        own = slice(ORIGIN, ORIGIN + self.size_z)
        around = self.near(self.vb, slot, ORIGIN, self.size_z)
        slot = self.at(slot)
        cross, last = [], []
        for c in range(self.count):
            ch = self.chunk(c)
            t = damping * self.u[slot, c, own] - around[c]
            t = jnp.where(self.gain[slot, c, own] > 0, t, 0.0)
            q = self.vb[slot, c, own]
            q_out[place + (slice(None), ch)] = q
            t_out[place + (slice(None), ch)] = t
            cross.append(w_ref[w_place + (slice(None), ch)] * q)
            last.append(q * t)
        dots[2] += self.folded(cross)
        dots[3] += self.folded(last)

    def folded(self, products):
        parts = [
            product[z0 : z0 + TILE] for product in products for z0 in range(0, self.size_z, TILE)
        ]
        while len(parts) > 1:
            parts = [sum(parts[k + 1 : k + 2], parts[k]) for k in range(0, len(parts), 2)]
        return parts[0]

    def handed(self):
        return (
            [(self.va, m) for m in range(1, 5)]
            + [(self.vb, m) for m in range(2, 6)]
            + [(self.u, m) for m in range(2, 5)]
            + [(self.gain, m) for m in range(1, 5)]
            + [(self.src, 1)]
        )


HANDED = 16


LEAD = 13
EDGE = 5


def each(first, end, stage, unroll=3):
    def body(x, carry):
        stage(x)
        return carry

    lax.fori_loop(first, end, body, 0, unroll=min(unroll, end - first))


def inner_steps(do, part, ls_ref, div_ref, act_ref, zl_ref, zh_ref, outs, dots):
    z_out, q_out, r_out, w_out, t_out = outs

    def own(x):
        do.own_plane(x, x, ls_ref, div_ref, act_ref, zl_ref, zh_ref, *part)

    def second(x):
        do.keep_first(x, x, (x,), div_ref, z_out, r_out, w_out, dots)
        do.smooth_second(x)

    def last(x):
        do.image_second(x, (x,), w_out, (x,), q_out, t_out, dots)

    def sweep(i):
        last(i - 8)
        second(i - 6)
        do.image_first(i - 4)
        do.smooth_first(i - 2)
        do.gains(i)
        own(i + 2)

    return own, second, last, sweep


def inner_first_kernel(dims, part, ls_ref, div_ref, act_ref, z_even, z_odd, *outs):
    vectors, hand_out, dots, fields = outs[:5], outs[5], outs[6], outs[7:]

    def run(odd):
        low, high = (z_odd, z_even) if odd == 0 else (z_even, z_odd)
        do = Stages(dims, RING, *fields)
        dots[...] = jnp.zeros_like(dots)
        own, second, _, sweep = inner_steps(
            do, part, ls_ref, div_ref, act_ref, low, high, vectors, dots
        )
        each(0, LEAD + 2, own)
        each(1, LEAD, do.gains)
        each(2, LEAD - 2, do.smooth_first)
        each(3, LEAD - 4, do.image_first)
        each(4, LEAD - 6, second)
        for item, (ref, m) in enumerate(do.handed()):
            hand_out[item] = ref[m]
        each(LEAD, part[1] - 2, sweep, 1)

    by_parity("gz", run)


def inner_last_kernel(
    dims, part, ls_ref, div_ref, act_ref, z_even, z_odd, w_first, dots_first, *refs
):
    held, vectors, hand_out, dots, fields = refs[:7], refs[7:12], refs[12], refs[13], refs[14:]
    size_x = dims[0]
    start, stop = part[0] - 2, size_x - 2

    def run(odd):
        low, high = (z_odd, z_even) if odd == 0 else (z_even, z_odd)
        do = Stages(dims, RING, *fields)
        dots[...] = dots_first[...]
        for ref, old, first, end in zip(
            fields, held, (-1, 0, -2, -8, -7, -9, -8), (2, 2, 2, 0, 0, -2, -2)
        ):
            for x in range(start + first, start + end):
                ref[x % RING] = old[x % RING]
        for x in range(start - 8, start - 6):
            vectors[3][x] = w_first[x]
        _, second, last, sweep = inner_steps(
            do, part, ls_ref, div_ref, act_ref, low, high, vectors, dots
        )
        each(start, stop, sweep, 1)
        each(stop, size_x - 1, do.gains)
        each(stop - 2, size_x - 2, do.smooth_first)
        each(stop - 4, size_x - 3, do.image_first)
        each(stop - 6, size_x - 4, second)
        each(stop - 8, size_x - 5, last)
        for item, (ref, m) in enumerate(do.handed()):
            hand_out[item] = ref[do.at(size_x - 1 - m)]

    by_parity("gz", run)


SPAN = 12


def ends_kernel(
    dims, parts, ls_ref, div_ref, act_ref, z_first_even, z_first_odd, z_last_even, z_last_odd, x_even, x_odd, c_even, c_odd,
    hand_low, hand_high, w_low, w_high, inner_dots, z_out, q_out, r_out, w_out, t_out, sums_out, dots, *fields,
):
    size_x, size_z, _ = dims
    z_first, z_last = (z_first_even, z_first_odd), (z_last_even, z_last_odd)
    do = Stages(dims, 0, *fields)
    dots[...] = inner_dots[...]

    def slot(side, m):
        return side * SPAN + m + DEEP

    def x_of(side, m):
        return m if side == 0 else size_x - 1 - m

    for side in range(2):
        for item, (ref, m) in enumerate(do.handed()):
            ref[slot(side, m)] = (hand_low, hand_high)[side][item]
        blank = jnp.zeros((TILE, LANES), f32)
        for c in range(do.count):
            do.open[slot(side, -DEEP), c, ORIGIN - TILE : ORIGIN] = blank
            do.open[slot(side, -DEEP), c, ORIGIN + size_z : ORIGIN + size_z + TILE] = blank

    def fill_z(odd):
        cl_ref, ch_ref = (c_odd, c_even) if odd == 0 else (c_even, c_odd)
        for side in range(2):
            z_even, z_odd = (z_first, z_last)[side]
            zl_ref, zh_ref = (z_odd, z_even) if odd == 0 else (z_even, z_odd)
            for m in range(2):
                do.own_plane(
                    slot(side, m), x_of(side, m), ls_ref, div_ref, act_ref, zl_ref, zh_ref, *parts[side]
                )
            flag = 2 * HALO * TILE + side
            for p in range(HALO):
                here = slot(side, p - HALO if side == 0 else -1 - p)
                row = (side * HALO + p) * TILE
                below, above = cl_ref[row : row + TILE], ch_ref[row : row + TILE]
                do.put_source(here, ORIGIN - HALO, below)
                do.put_source(here, ORIGIN + size_z - HALO, above)
                do.put(here, ORIGIN - TILE, below, do.spread(cl_ref[flag : flag + 1]))
                do.put(here, ORIGIN + size_z, above, do.spread(ch_ref[flag : flag + 1]))

    def fill_x(odd):
        for side, ref in enumerate((x_odd, x_even) if odd == 0 else (x_even, x_odd)):
            flags = (DEEP + HALO) * size_z
            for p in range(DEEP):
                here = slot(side, p - DEEP if side == 0 else -1 - p)
                for j in range(size_z // TILE):
                    row = p * size_z + j * TILE
                    act = do.spread(ref[flags + j : flags + j + 1])
                    do.put(here, ORIGIN + j * TILE, ref[row : row + TILE], act)
            for p in range(HALO):
                row = (DEEP + p) * size_z
                here = slot(side, p - HALO if side == 0 else -1 - p)
                do.put_source(here, ORIGIN, ref[row : row + size_z])

    by_parity("gz", fill_z)
    by_parity("gx", fill_x)

    def both(first, end, stage):
        def body(n, carry):
            for side in range(2):
                stage(side, side * SPAN + n, n - DEEP)
            return carry

        lax.fori_loop(first + DEEP, end + DEEP, body, 0)

    both(-4, 1, lambda side, here, m: do.gains(here))
    both(-3, 2, lambda side, here, m: do.smooth_first(here))
    both(-2, 3, lambda side, here, m: do.image_first(here))
    both(
        0, EDGE - 1,
        lambda side, here, m: do.keep_first(
            here, x_of(side, m), (side, m), div_ref, z_out, r_out, w_out, dots
        ),
    )
    for side in range(2):
        w_out[side, EDGE - 1] = (w_low, w_high)[side][x_of(side, EDGE - 1)]
    both(-1, 4, lambda side, here, m: do.smooth_second(here))
    both(
        0, EDGE,
        lambda side, here, m: do.image_second(
            here, (side, m), w_out, (side, m), q_out, t_out, dots
        ),
    )
    lane = lax.broadcasted_iota(jnp.int32, (1, LANES), 1)
    line = jnp.zeros((1, LANES), f32)
    for place in range(4):
        line = jnp.where(lane == place, jnp.sum(dots[place]), line)
    sums_out[...] = jnp.broadcast_to(line, sums_out.shape)


def final_kernel(
    planes, meet, sums_ref, *refs
):
    first, final, ends = refs[:5], refs[5:10], refs[10:15]
    pressure_out, residual_out, pressure, residual, sems = refs[15:]
    totals = jnp.sum(sums_ref[...], axis=0, keepdims=True)
    lane = lax.broadcasted_iota(jnp.int32, totals.shape, 1)
    gamma, delta, cross, last = [
        jnp.sum(jnp.where(lane == place, totals, 0.0), axis=1, keepdims=True) for place in range(4)
    ]
    alpha = gamma / delta
    gamma_next = gamma - 2.0 * alpha * delta + alpha * alpha * cross
    beta = gamma_next / gamma
    delta_next = delta - 2.0 * alpha * cross + alpha * alpha * last
    alpha_next = gamma_next / (delta_next - beta * gamma_next / alpha)
    size_x, _, size_y = pressure.shape
    on_first = jnp.broadcast_to(alpha + alpha_next * (1.0 + beta), (1, LANES))
    on_second = jnp.broadcast_to(-alpha_next * alpha, (1, LANES))
    on_first = jnp.concatenate([on_first] * (size_y // LANES), 1)
    on_second = jnp.concatenate([on_second] * (size_y // LANES), 1)

    def put(x, z, q, r, w, t):
        pressure[x] = on_first * z + on_second * q
        residual[x] = r - on_first * w - on_second * t

    late = (0, 2, 0, 0, 2)

    def one(x):
        edge = min(x, size_x - 1 - x)
        side = int(x >= size_x // 2)
        picked = []
        for k in range(5):
            if edge < (EDGE if late[k] else EDGE - 1):
                picked.append(ends[k][side, edge])
            else:
                picked.append((first if x < meet - late[k] else final)[k][x])
        put(x, *picked)

    for x in (*range(EDGE), meet - 2, meet - 1, *range(size_x - EDGE, size_x)):
        one(x)

    def from_first(x, carry):
        put(x, *(ref[x] for ref in first))
        return carry

    def from_final(x, carry):
        put(x, *(ref[x] for ref in final))
        return carry

    copies = []
    for chunk in range(size_x // planes):
        begin, end = chunk * planes, (chunk + 1) * planes
        for low, high, step in ((EDGE, meet - 2, from_first), (meet, size_x - EDGE, from_final)):
            low, high = max(begin, low), min(end, high)
            if low < high:
                lax.fori_loop(low, high, step, 0, unroll=min(4, high - low))
        where = pl.ds(begin, planes)
        for place, (src, dst) in enumerate(((pressure, pressure_out), (residual, residual_out))):
            copy = pltpu.make_async_copy(src.at[where], dst.at[where], sems.at[2 * chunk + place])
            copy.start()
            copies.append(copy)
    for copy in copies:
        copy.wait()


def exchange(values, axis, odd):
    count = lax.axis_size(axis)
    pairs = [(i, ((i - odd) ^ 1) + odd) for i in range(count)]
    return lax.ppermute(values, axis, [(i, j) for i, j in pairs if 0 <= j < count])


def on_device(divergence, level_set, tile_ids):
    dims = divergence.shape
    size_x, size_z, size_y = dims
    tiles_x, tiles_z = size_x // TILE, size_z // TILE
    count_x, count_z = lax.axis_size("gx"), lax.axis_size("gz")

    half = tiles_x // 2 * TILE
    parts = ((0, half), (half, size_x - half))
    z_rows = [span * TILE + span + -(-span // TILE // TILE) * TILE for _, span in parts]
    x_rows = (DEEP + HALO) * size_z + TILE
    c_rows = 2 * HALO * TILE + TILE
    x_even, x_odd, act = pl.pallas_call(
        functools.partial(pack_x_kernel, dims),
        out_shape=(array(x_rows, size_y),) * 2 + (array(tiles_z, tiles_x, size_y),),
        in_specs=[HBM_SPEC] * 3,
        out_specs=(VMEM_SPEC,) * 3,
        scratch_shapes=[
            pltpu.VMEM(tile_ids.shape, jnp.int32),
            pltpu.VMEM((2 * (DEEP + HALO), size_z, size_y), f32),
            pltpu.SemaphoreType.DMA((5,)),
        ],
        compiler_params=limit(57),
        name="pack_x",
    )(tile_ids, level_set, divergence)
    x_even = exchange(x_even, "gx", 0)
    x_odd = exchange(x_odd, "gx", 1)
    sent = pl.pallas_call(
        functools.partial(pack_z_kernel, dims, parts),
        out_shape=[array(rows, size_y) for rows in z_rows for _ in range(2)],
        in_specs=[VMEM_SPEC] * 3,
        out_specs=[VMEM_SPEC] * 4,
        compiler_params=limit(8),
        name="pack_z",
    )(level_set, divergence, act)
    z_first, z_last = [
        (exchange(sent[2 * part], "gz", 0), exchange(sent[2 * part + 1], "gz", 1))
        for part in range(2)
    ]

    def fields(planes):
        return [pltpu.VMEM((planes, size_y // LANES, size_z + ROWS, LANES), f32)] * 7

    block = array(*dims)
    chunks, rows = size_y // LANES, size_z + ROWS
    hand = array(HANDED, chunks, rows, LANES)
    dots = array(4, TILE, LANES)
    ring = [array(RING, chunks, rows, LANES)] * 7
    early = array(half, size_z, size_y)
    first_call = pl.pallas_call(
        functools.partial(inner_first_kernel, dims, parts[0]),
        out_shape=[early] * 5 + [hand, dots] + ring,
        in_specs=[VMEM_SPEC] * 5,
        out_specs=[VMEM_SPEC] * 14,
        compiler_params=limit(4),
        name="inner_first",
    )
    *first, hand_low, dots_first = (outs := first_call(level_set, divergence, act, *z_first))[:7]
    held = outs[7:]
    c_even, c_odd = pl.pallas_call(
        functools.partial(pack_corner_kernel, dims),
        out_shape=(array(c_rows, size_y),) * 2,
        in_specs=[VMEM_SPEC] * 3,
        out_specs=(VMEM_SPEC,) * 2,
        compiler_params=limit(8),
        name="pack_corner",
    )(x_even, x_odd, dots_first)
    c_odd = exchange(c_odd, "gz", 1)
    c_even = exchange(c_even, "gz", 0)

    last_call = pl.pallas_call(
        functools.partial(inner_last_kernel, dims, parts[1]),
        out_shape=[block] * 5 + [hand, dots],
        in_specs=[VMEM_SPEC] * 14,
        out_specs=[VMEM_SPEC] * 7,
        scratch_shapes=fields(RING),
        compiler_params=limit(12),
        name="inner_last",
    )
    *second, hand_high, dots_last = last_call(
        level_set, divergence, act, *z_last, first[3], dots_first, *held
    )

    devices = count_x * count_z
    end = array(2, EDGE, size_z, size_y)
    *ends, sums = pl.pallas_call(
        functools.partial(ends_kernel, dims, parts),
        out_shape=(end,) * 5 + (array(devices, LANES),),
        in_specs=[VMEM_SPEC] * 16,
        out_specs=(VMEM_SPEC,) * 6,
        scratch_shapes=[pltpu.VMEM((4, TILE, LANES), f32)] + fields(2 * SPAN),
        compiler_params=limit(20),
        name="ends",
    )(
        level_set, divergence, act, *z_first, *z_last, x_even, x_odd, c_even, c_odd,
        hand_low, hand_high, first[3], second[3], dots_last,
    )

    gathered = lax.all_to_all(sums, ("gx", "gz"), 0, 0, tiled=True)
    planes = TILE
    return tuple(
        pl.pallas_call(
            functools.partial(final_kernel, planes, half - 8),
            out_shape=(block,) * 2,
            in_specs=[VMEM_SPEC] * 16,
            out_specs=(HBM_SPEC,) * 2,
            scratch_shapes=[
                pltpu.VMEM(dims, f32),
                pltpu.VMEM(dims, f32),
                pltpu.SemaphoreType.DMA((2 * size_x // planes,)),
            ],
            compiler_params=limit(8),
            name="outputs",
        )(gathered, *first, *second, *ends)
    )


def solution(mesh):
    placed = (P("gx", "gz", None), P("gx", "gz", None), P("gx", "gz"))
    return jax.shard_map(
        on_device,
        mesh=mesh,
        in_specs=placed,
        out_specs=(P("gx", "gz", None), P("gx", "gz", None)),
        check_vma=False,
    )
```

time: 273 us -> 61 us (0.22)
  blocking collectives: 90.4 us -> 17.7 us
  other arithmetic: 48.8 us -> 0 us
  local copies, waits for them, and re-layouts: 47 us -> 0.84 us
  starting transfers between devices: 52.2 us -> 13.8 us
  Pallas kernels: 0 us -> 27.5 us
  waiting for transfers between devices: 27.1 us -> 0.02 us
  between operations: 6.58 us -> 0.81 us
    psum x2 -> x0, blocking collectives: 90.4 us -> none  [both_sums(): lax.psum((jnp.sum(current * preconditioned), jnp.sum(image_of * precondit...]
    ppermute x20 -> x8, starting transfers between devices: 52.2 us -> 13.8 us  [exchange(): lax.ppermute(values, axis, [(i, j) for i, j in pairs if 0 <= j < count])]
    pallas_call x0 -> x7, Pallas kernels: none -> 27.5 us  [the longest x1 11 us: on_device(): last_call(level_set, divergence, act, *z_last, first[3], dots_first, *held)]
    ppermute x20 -> x8, waiting for transfers between devices: 27.1 us -> 0.02 us  [exchange(): lax.ppermute(values, axis, [(i, j) for i, j in pairs if 0 <= j < count])]
    reshape x1 -> x0, local copies, waits for them, and re-layouts: 25.1 us -> none  [on_device(): active = jnp.broadcast_to(listed_hit[:, None, :, None, :, None], (tiles_x...]
    all_to_all x0 -> x1, blocking collectives: none -> 17.7 us  [on_device(): gathered = lax.all_to_all(sums, ('gx', 'gz'), 0, 0, tiled=True)]
    add x3 -> x0, other arithmetic: 12.8 us -> none  [the longest x2 8.42 us: precondition(): second_pass = first_pass + scale_mid * (residual - operate(first_pass))]
    mul x2 -> x0, other arithmetic: 12.3 us -> none  [precondition(): first_pass = scale_mid * residual]
  transfers between devices with their start and end apart: 20 -> 8, of which waited for: 13 -> 0; matrix products, arithmetic and copies ran while one was open for 1% -> 0% of each run, Pallas kernels for 0% -> 30%
where the time goes in v1:
time: 61 us; the launch traced here: 60.6 us
  Pallas kernels  27.5 us (45%)
  blocking collectives  17.7 us (29%)
  starting transfers between devices  13.8 us (23%)
  local copies, waits for them, and re-layouts  0.84 us (1%)
  between operations  0.81 us (1%)
    all_to_all x1, blocking collectives, on_device(): gathered = lax.all_to_all(sums, ('gx', 'gz'), 0, 0, tiled=True)  17.7 us
    ppermute x8, starting transfers between devices, exchange(): lax.ppermute(values, axis, [(i, j) for i, j in pairs if 0 <= j < count])  13.8 us
    pallas_call x1, Pallas kernels, on_device(): last_call(level_set, divergence, act, *z_last, first[3], dots_first, *held)  11 us
    pallas_call x1, Pallas kernels, on_device(): first_call(level_set, divergence, act, *z_first)  7.45 us
    pallas_call x1, Pallas kernels, on_device(): pl.pallas_call(functools.partial(ends_kernel, dims, parts), out_shape=(en...  3.81 us
    pallas_call x1, Pallas kernels, on_device(): pl.pallas_call(functools.partial(pack_x_kernel, dims), out_shape=(array(x...  2.42 us
    pallas_call x1, Pallas kernels, on_device(): pl.pallas_call(functools.partial(final_kernel, planes, half - 8), out_sha...  2.37 us
  transfers between devices with their start and end apart: 8, of which 0 were waited for; matrix products, arithmetic and copies ran while one was open for 0% of the time, Pallas kernels for 30%

profile of v1, /device:TPU:0, one launch (start us, length us, event | category | flops | bytes accessed | tf_op | source)
XLA Modules:
  0.0 60.6 jit_solution(1416866339850680053)
XLA Ops:
  0.6 0.0 copy-start.1
  0.6 0.0 copy-start
  0.6 2.4 %pack_x.1 = (f32[152,512]{1,0:T(8,128)}, f32[152,512]{1,0:T(8,128)}, f32[2,8,512]{2,1,0:T(8,128)}) custom-call(s32[1,1024]{1,0:T(1,128)} %ids_hbm.1, f32[64,16,512]{2,1,0:T(8,128)} %ls_ref.7, f32[64,16,512]{2,1,0:T(8,128)} %div_ref.7), custom_call_target="tpu_custom_call" | custom-call | tf_op jit(solution)/shard_map/pack_x/pallas_call | solution.py:625
  3.1 0.0 copy-done.1
  3.1 0.1 copy-done
  3.2 0.0 copy-start.2
  3.2 0.8 %copy-done.2 = f32[2,8,512]{2,1,0:T(8,128)S(1)} copy-done((f32[2,8,512]{2,1,0:T(8,128)S(1)}, f32[2,8,512]{2,1,0:T(8,128)}, u32[]{:S(2)}) %copy-start.2) | copy-done | bytes 32792
  3.9 0.0 copy-start.5
  3.9 0.0 copy-start.4
  3.9 0.4 pack_z.1
  4.3 0.5 collective-permute-start
  4.9 0.7 %collective-permute-start.1 = (f32[296,512]{1,0:T(8,128)S(1)}, f32[296,512]{1,0:T(8,128)S(1)}, u32[]{:S(2)}, u32[]{:S(2)}) collective-permute-start(f32[296,512]{1,0:T(8,128)S(1)} %get-tuple-element.40), channel_id=1, source_target_pairs={{1,2},{2,1},{3,4},{4,3},{5,6},{6,5},{9,10},{10,9},{11,12},{12,11},... | collective-permute-start | bytes 1818632 | tf_op jit(solution)/shard_map/ppermute | solution.py:611
  5.6 4.0 %collective-permute-start.2 = (f32[296,512]{1,0:T(8,128)S(1)}, f32[296,512]{1,0:T(8,128)S(1)}, u32[]{:S(2)}, u32[]{:S(2)}) collective-permute-start(f32[296,512]{1,0:T(8,128)S(1)} %get-tuple-element.41), channel_id=1, source_target_pairs={{0,1},{1,0},{2,3},{3,2},{4,5},{5,4},{6,7},{7,6},{8,9},{9,8},{10,11... | collective-permute-start | bytes 1818632 | tf_op jit(solution)/shard_map/ppermute | solution.py:611
  9.5 0.7 %collective-permute-start.3 = (f32[296,512]{1,0:T(8,128)S(1)}, f32[296,512]{1,0:T(8,128)S(1)}, u32[]{:S(2)}, u32[]{:S(2)}) collective-permute-start(f32[296,512]{1,0:T(8,128)S(1)} %get-tuple-element.42), channel_id=1, source_target_pairs={{1,2},{2,1},{3,4},{4,3},{5,6},{6,5},{9,10},{10,9},{11,12},{12,11},... | collective-permute-start | bytes 1818632 | tf_op jit(solution)/shard_map/ppermute | solution.py:611
  10.2 0.0 copy-done.5
  10.3 1.6 %collective-permute-start.4 = (f32[152,512]{1,0:T(8,128)S(1)}, f32[152,512]{1,0:T(8,128)S(1)}, u32[]{:S(2)}, u32[]{:S(2)}) collective-permute-start(f32[152,512]{1,0:T(8,128)S(1)} %copy-done.5), channel_id=1, source_target_pairs={{0,8},{8,0},{16,24},{24,16},{1,9},{9,1},{17,25},{25,17},{2,10},{10... | collective-permute-start | bytes 933896 | tf_op jit(solution)/shard_map/ppermute | solution.py:611
  11.8 0.0 collective-permute-done.z_even.z_first_even
  11.8 0.0 copy-done.4
  11.8 0.0 copy-start.3
  11.8 0.8 %collective-permute-start.5 = (f32[152,512]{1,0:T(8,128)S(1)}, f32[152,512]{1,0:T(8,128)S(1)}, u32[]{:S(2)}, u32[]{:S(2)}) collective-permute-start(f32[152,512]{1,0:T(8,128)S(1)} %copy-done.4), channel_id=1, source_target_pairs={{8,16},{16,8},{9,17},{17,9},{10,18},{18,10},{11,19},{19,11},{12,20... | collective-permute-start | bytes 933896 | tf_op jit(solution)/shard_map/ppermute | solution.py:611
  12.6 0.0 collective-permute-done.1.z_odd.z_first_odd
  12.6 7.4 %inner_first.1 = (f32[32,16,512]{2,1,0:T(8,128)S(1)}, f32[32,16,512]{2,1,0:T(8,128)S(1)}, f32[32,16,512]{2,1,0:T(8,128)S(1)}, f32[32,16,512]{2,1,0:T(8,128)S(1)}...) custom-call(f32[64,16,512]{2,1,0:T(8,128)S(1)} %copy-done, ...), custom_call_target="tpu_custom_call" | custom-call | tf_op jit(solution)/shard_map/inner_first/pallas_call | solution.py:670
  20.1 0.0 collective-permute-done.4.x_even
  20.1 0.0 collective-permute-done.5.x_odd
  20.1 0.1 pack_corner.1
  20.2 4.9 %collective-permute-start.6 = (f32[72,512]{1,0:T(8,128)S(1)}, f32[72,512]{1,0:T(8,128)S(1)}, u32[]{:S(2)}, u32[]{:S(2)}) collective-permute-start(f32[72,512]{1,0:T(8,128)S(1)} %get-tuple-element.46), channel_id=1, source_target_pairs={{0,1},{1,0},{2,3},{3,2},{4,5},{5,4},{6,7},{7,6},{8,9},{9,8},{10,11... | collective-permute-start | bytes 442376 | tf_op jit(solution)/shard_map/ppermute | solution.py:611
  25.1 0.7 %collective-permute-start.7 = (f32[72,512]{1,0:T(8,128)S(1)}, f32[72,512]{1,0:T(8,128)S(1)}, u32[]{:S(2)}, u32[]{:S(2)}) collective-permute-start(f32[72,512]{1,0:T(8,128)S(1)} %get-tuple-element.47), channel_id=1, source_target_pairs={{1,2},{2,1},{3,4},{4,3},{5,6},{6,5},{9,10},{10,9},{11,12},{12,11},... | collective-permute-start | bytes 442376 | tf_op jit(solution)/shard_map/ppermute | solution.py:611
  25.8 0.0 collective-permute-done.2.z_even.z_last_even
  25.8 0.0 collective-permute-done.3.z_odd.z_last_odd
  25.8 0.0 copy-done.3
  25.8 11.0 %inner_last.1 = (f32[64,16,512]{2,1,0:T(8,128)S(1)}, f32[64,16,512]{2,1,0:T(8,128)S(1)}, f32[64,16,512]{2,1,0:T(8,128)S(1)}, f32[64,16,512]{2,1,0:T(8,128)S(1)},...) custom-call(f32[64,16,512]{2,1,0:T(8,128)S(1)} %copy-done, ...), custom_call_target="tpu_custom_call" | custom-call | tf_op jit(solution)/shard_map/inner_last/pallas_call | solution.py:692
  36.8 0.0 collective-permute-done.6.c_even
  36.8 0.0 collective-permute-done.7.c_odd
  36.8 3.8 %ends.1 = (f32[2,5,16,512]{3,2,1,0:T(8,128)S(1)}, f32[2,5,16,512]{3,2,1,0:T(8,128)S(1)}, f32[2,5,16,512]{3,2,1,0:T(8,128)S(1)}, f32[2,5,16,512]{3,2,1,0:T(8,128)...) custom-call(f32[64,16,512]{2,1,0:T(8,128)S(1)} %copy-done, f32[64,16,512]{2,1,0:T(8,128)S(1)} %copy-done.1, ...), custom_call_target="tpu_custom_call" | custom-call | tf_op jit(solution)/shard_map/ends/pallas_call | solution.py:698
  40.6 17.7 %all_to_all.11 = f32[32,1,128]{2,1,0:T(1,128)S(1)} all-to-all(f32[32,1,128]{2,1,0:T(1,128)S(1)} %bitcast.5), channel_id=1, replica_groups=mesh['gx'=4,'gz'=8] {'gx','gz'}, dimensions={0} | all-to-all | bytes 32768 | tf_op jit(solution)/shard_map/all_to_all | solution.py:711
  58.3 2.4 %outputs.1 = (f32[64,16,512]{2,1,0:T(8,128)}, f32[64,16,512]{2,1,0:T(8,128)}) custom-call(f32[32,128]{1,0:T(8,128)S(1)} %bitcast.4, f32[32,16,512]{2,1,0:T(8,128)S(1)} %get-tuple-element.61.refs_0_, f32[32,16,512]{2,1,0:T(8,128)S(1)} %get-tuple-element.62.refs_1_, f32[32,16,512]{2,1,0:T(8,128)S(1)} %get-tuple-element.63.refs_2_, ...), custom_call_target="tpu_custom_call" | custom-call | tf_op jit(solution)/shard_map/outputs/pallas_call | solution.py:714
Async XLA Ops:
  0.6 2.4 %copy-start.1 = (f32[64,16,512]{2,1,0:T(8,128)S(1)}, f32[64,16,512]{2,1,0:T(8,128)}, u32[]{:S(2)}) copy-start(f32[64,16,512]{2,1,0:T(8,128)} %div_ref.7) | copy-start | bytes 6291460
  0.6 2.5 %copy-start = (f32[64,16,512]{2,1,0:T(8,128)S(1)}, f32[64,16,512]{2,1,0:T(8,128)}, u32[]{:S(2)}) copy-start(f32[64,16,512]{2,1,0:T(8,128)} %ls_ref.7) | copy-start | bytes 6291460
  3.2 0.8 %copy-start.2 = (f32[2,8,512]{2,1,0:T(8,128)S(1)}, f32[2,8,512]{2,1,0:T(8,128)}, u32[]{:S(2)}) copy-start(f32[2,8,512]{2,1,0:T(8,128)} %get-tuple-element.38.act_ref) | copy-start | bytes 98308
  3.9 6.3 %copy-start.5 = (f32[152,512]{1,0:T(8,128)S(1)}, f32[152,512]{1,0:T(8,128)}, u32[]{:S(2)}) copy-start(f32[152,512]{1,0:T(8,128)} %get-tuple-element.43) | copy-start | bytes 933892
  3.9 7.9 %copy-start.4 = (f32[152,512]{1,0:T(8,128)S(1)}, f32[152,512]{1,0:T(8,128)}, u32[]{:S(2)}) copy-start(f32[152,512]{1,0:T(8,128)} %get-tuple-element.44) | copy-start | bytes 933892
  4.3 7.5 %collective-permute-start = (f32[296,512]{1,0:T(8,128)S(1)}, f32[296,512]{1,0:T(8,128)S(1)}, u32[]{:S(2)}, u32[]{:S(2)}) collective-permute-start(f32[296,512]{1,0:T(8,128)S(1)} %get-tuple-element.39), channel_id=1, source_target_pairs={{0,1},{1,0},{2,3},{3,2},{4,5},{5,4},{6,7},{7,6},{8,9},{9,8},{10,11... | collective-permute-start | bytes 1818632 | tf_op jit(solution)/shard_map/ppermute | solution.py:611
  4.9 7.8 %collective-permute-start.1 = (f32[296,512]{1,0:T(8,128)S(1)}, f32[296,512]{1,0:T(8,128)S(1)}, u32[]{:S(2)}, u32[]{:S(2)}) collective-permute-start(f32[296,512]{1,0:T(8,128)S(1)} %get-tuple-element.40), channel_id=1, source_target_pairs={{1,2},{2,1},{3,4},{4,3},{5,6},{6,5},{9,10},{10,9},{11,12},{12,11},... | collective-permute-start | bytes 1818632 | tf_op jit(solution)/shard_map/ppermute | solution.py:611
  5.6 20.2 %collective-permute-start.2 = (f32[296,512]{1,0:T(8,128)S(1)}, f32[296,512]{1,0:T(8,128)S(1)}, u32[]{:S(2)}, u32[]{:S(2)}) collective-permute-start(f32[296,512]{1,0:T(8,128)S(1)} %get-tuple-element.41), channel_id=1, source_target_pairs={{0,1},{1,0},{2,3},{3,2},{4,5},{5,4},{6,7},{7,6},{8,9},{9,8},{10,11... | collective-permute-start | bytes 1818632 | tf_op jit(solution)/shard_map/ppermute | solution.py:611
  9.5 16.2 %collective-permute-start.3 = (f32[296,512]{1,0:T(8,128)S(1)}, f32[296,512]{1,0:T(8,128)S(1)}, u32[]{:S(2)}, u32[]{:S(2)}) collective-permute-start(f32[296,512]{1,0:T(8,128)S(1)} %get-tuple-element.42), channel_id=1, source_target_pairs={{1,2},{2,1},{3,4},{4,3},{5,6},{6,5},{9,10},{10,9},{11,12},{12,11},... | collective-permute-start | bytes 1818632 | tf_op jit(solution)/shard_map/ppermute | solution.py:611
  10.3 9.8 %collective-permute-start.4 = (f32[152,512]{1,0:T(8,128)S(1)}, f32[152,512]{1,0:T(8,128)S(1)}, u32[]{:S(2)}, u32[]{:S(2)}) collective-permute-start(f32[152,512]{1,0:T(8,128)S(1)} %copy-done.5), channel_id=1, source_target_pairs={{0,8},{8,0},{16,24},{24,16},{1,9},{9,1},{17,25},{25,17},{2,10},{10... | collective-permute-start | bytes 933896 | tf_op jit(solution)/shard_map/ppermute | solution.py:611
  11.8 14.0 %copy-start.3 = (f32[2,8,512]{2,1,0:T(8,128)S(1)}, f32[2,8,512]{2,1,0:T(8,128)}, u32[]{:S(2)}) copy-start(f32[2,8,512]{2,1,0:T(8,128)} %get-tuple-element.38.act_ref) | copy-start | bytes 98308
  11.8 8.3 %collective-permute-start.5 = (f32[152,512]{1,0:T(8,128)S(1)}, f32[152,512]{1,0:T(8,128)S(1)}, u32[]{:S(2)}, u32[]{:S(2)}) collective-permute-start(f32[152,512]{1,0:T(8,128)S(1)} %copy-done.4), channel_id=1, source_target_pairs={{8,16},{16,8},{9,17},{17,9},{10,18},{18,10},{11,19},{19,11},{12,20... | collective-permute-start | bytes 933896 | tf_op jit(solution)/shard_map/ppermute | solution.py:611
  20.2 16.6 %collective-permute-start.6 = (f32[72,512]{1,0:T(8,128)S(1)}, f32[72,512]{1,0:T(8,128)S(1)}, u32[]{:S(2)}, u32[]{:S(2)}) collective-permute-start(f32[72,512]{1,0:T(8,128)S(1)} %get-tuple-element.46), channel_id=1, source_target_pairs={{0,1},{1,0},{2,3},{3,2},{4,5},{5,4},{6,7},{7,6},{8,9},{9,8},{10,11... | collective-permute-start | bytes 442376 | tf_op jit(solution)/shard_map/ppermute | solution.py:611
  25.1 11.7 %collective-permute-start.7 = (f32[72,512]{1,0:T(8,128)S(1)}, f32[72,512]{1,0:T(8,128)S(1)}, u32[]{:S(2)}, u32[]{:S(2)}) collective-permute-start(f32[72,512]{1,0:T(8,128)S(1)} %get-tuple-element.47), channel_id=1, source_target_pairs={{1,2},{2,1},{3,4},{4,3},{5,6},{6,5},{9,10},{10,9},{11,12},{12,11},... | collective-permute-start | bytes 442376 | tf_op jit(solution)/shard_map/ppermute | solution.py:611
